TPU v7x, 32 devices: a whole 2x2x4 slice. The times are simulated.
32 devices in a mesh: tm: 32 (over z, y, x, core).
Axes of the slice: x: 2, y: 2, z: 4, core: 2. Of those that a mesh axis runs over, the one named last changes fastest.
Arguments:
- krylov_basis: float32 [8, 128, 32, 512], P(None, 'tm'), may hold values from -6 to 6, as said below
- vector: float32 [128, 32, 512], P('tm'), may hold values from -60 to 60
- conductance: float32 [32, 512], replicated, may hold values from 1e-05 to 0.3
Outputs:
- preconditioned: float32 [128, 32, 512], P('tm')
- next_vector: float32 [128, 32, 512], P('tm')
- coefficients: float32 [9], replicated
Inputs may be any that keep to these rules, and one draw needn't show every extreme that they name: `krylov_basis`: the 8 fields are orthonormal, up to float32 rounding, under the mean over all cells of their product.
All inputs are finite; a program needn't handle non-finite values.
Results may differ from a plain program's by a relative error of at most 0.0003.
Values sent between devices are 32-bit elements.
A program may use at most 64 MiB of HBM per device.

v0:
```python
import jax
import jax.numpy as jnp
from jax import lax
from jax.sharding import PartitionSpec as P

LEVELS = 3


OMEGA = 0.7
FLOOR = 0.25


def passed_along(value, axis, steps):
    count = lax.axis_size(axis)
    initial, last = (max(0, -steps), min(count, count - steps))
    return lax.ppermute(value, axis, [(source, source + steps) for source in range(initial, last)])


def entering(value, axis, combine, identity):
    length, mine = (lax.axis_size(axis), lax.axis_index(axis))
    everything = jax.tree.map(lambda part: lax.all_gather(part, axis), value)
    start = jax.tree.map(
        lambda part, zero: jnp.broadcast_to(jnp.asarray(zero, part.dtype), part.shape),
        value,
        identity,
    )

    def lap(k, before):
        reached = k < mine
        new = combine(before, jax.tree.map(lambda part: part[k], everything))
        return jax.tree.map(lambda a, b: jnp.where(reached, a, b), new, before)

    return lax.fori_loop(0, length, lap, start)


def beside(volume):
    padded = jnp.pad(volume, ((0, 0), (1, 1), (1, 1)))
    return padded[:, 2:, 1:-1] + padded[:, :-2, 1:-1] + padded[:, 1:-1, 2:] + padded[:, 1:-1, :-2]


def spatial(volume, conduct):
    return volume + conduct * (4.0 * volume - beside(volume))


def time_operator(volume, conduct):
    incoming = passed_along(volume[-1], "tm", 1)
    earlier = jnp.concatenate([incoming[None], volume[:-1]], axis=0)
    return spatial(volume, conduct) - earlier


def block_inverse(source, conduct):
    diagonal = 1.0 + 4.0 * conduct
    sweep_one = source / diagonal
    return (source + conduct * beside(sweep_one)) / diagonal


def march_from(entry, source, diagonal):

    def advance(carry_state, slab_in):
        carry_state = (slab_in + carry_state) / diagonal
        return (carry_state, carry_state)

    return lax.scan(advance, entry, source)[1]


def coarse_solve(source, conduct):
    diagonal = 1.0 + 4.0 * conduct
    nothing = jnp.zeros_like(conduct)
    partial_march = march_from(nothing, source, diagonal)
    slabs = source.shape[0]
    damping = 1.0 / diagonal
    factor = damping**slabs

    def combine_pair(earlier, following):
        return (earlier[0] * following[0], following[0] * earlier[1] + following[1])

    carried = entering(
        (factor, partial_march[-1]), "tm", combine_pair, (jnp.ones_like(conduct), nothing)
    )
    entry = carried[1]
    return march_from(entry, source, diagonal)


def vcycle(source, conduct, level_at):
    if level_at == LEVELS - 1:
        return coarse_solve(source, conduct)
    smooth = OMEGA * block_inverse(source, conduct)
    remain = source - time_operator(smooth, conduct)
    coarse = remain[0::2] + remain[1::2]
    correction = vcycle(coarse, 2.0 * conduct, level_at + 1)
    smooth = smooth + jnp.repeat(correction, 2, axis=0)
    return smooth + OMEGA * block_inverse(source - time_operator(smooth, conduct), conduct)


def on_device(krylov_basis, vector, conductance):
    count_all = vector.shape[0] * lax.axis_size("tm") * vector.shape[1] * vector.shape[2]
    preconditioned = vcycle(vector, conductance, 0)
    applied = time_operator(preconditioned, conductance)
    partial_dots = jnp.einsum("kabc,abc->k", krylov_basis, applied, precision=lax.Precision.HIGHEST)
    weights = lax.psum(partial_dots, "tm") / count_all
    applied = applied - jnp.einsum(
        "k,kabc->abc", weights, krylov_basis, precision=lax.Precision.HIGHEST
    )
    length = jnp.sqrt(lax.psum(jnp.sum(applied * applied), "tm") / count_all)
    next_vector = applied / jnp.maximum(length, FLOOR)
    coefficients = jnp.concatenate([weights, length[None]])
    return (preconditioned, next_vector, coefficients)


def solution(mesh):
    in_specs = (P(None, "tm", None, None), P("tm", None, None), P())
    out_specs = (P("tm", None, None), P("tm", None, None), P())
    return jax.shard_map(
        on_device, mesh=mesh, in_specs=in_specs, out_specs=out_specs, check_vma=False
    )
```

profile of v0, /device:TPU:0, one launch (start us, length us, event | category | flops | bytes accessed | tf_op | source)
XLA Modules:
  0.0 290.9 jit_solution(240442995683912266)
XLA Ops:
  7.2 1.0 broadcast_multiply_fusion.2
  8.3 1.0 broadcast_divide_fusion.2
  9.2 1.2 broadcast_multiply_fusion
  10.4 2.4 collective-permute-start
  14.1 4.9 %collective-permute-start.1 = (f32[32,512]{1,0:T(8,128)S(1)}, f32[32,512]{1,0:T(8,128)S(1)}, u32[]{:S(2)}, u32[]{:S(2)}) collective-permute-start(f32[32,512]{1,0:T(8,128)S(1)} %get-tuple-element.168), channel_id=1, source_target_pairs={{0,1},{1,2},{2,3},{3,4},{4,5},{5,6},{6,7},{7,8},{8,9},{9,10},{10,1... | collective-permute-start | bytes 196616 | tf_op jit(solution)/shard_map/ppermute | solution.py:16
  19.1 0.9 collective-permute-done.1
  21.6 62.1 %all-gather.5.cloned.1.call-done = f32[1024,512]{1,0:T(8,128)} async-done(((f32[32,512]{1,0:T(8,128)}), f32[1024,512]{1,0:T(8,128)}) %all-gather.5.cloned.1.call-update) | async-done | bytes 2097168 | tf_op jit(solution)/shard_map/all_gather | solution.py:21
  83.7 58.5 %all-gather.7.cloned.1.call-done = f32[1024,512]{1,0:T(8,128)} async-done(((f32[32,512]{1,0:T(8,128)}), f32[1024,512]{1,0:T(8,128)}) %all-gather.7.cloned.1.call-update) | async-done | bytes 2097168 | tf_op jit(solution)/shard_map/all_gather | solution.py:21
  142.2 30.0 %while.9 = (s32[]{:T(128)}, f32[32,512]{1,0:T(8,128)S(1)}, s32[]{:T(128)}, f32[32,32,512]{2,1,0:T(8,128)}, f32[32,32,512]{2,1,0:T(8,128)}, /*index=5*/s32[]{:T(128)}, s32[]{:T(128)}) while((s32[]{:T(128)}, f32[32,512]{1,0:T(8,128)S(1)}, s32[]{:T(128)}, f32[32,32,512]{2,1,0:T(8,128)}, f32[32,32,512]{2,1,0:T(8,128)}, ...), condition=%wide.region_1.2_spmd.clone, body=%wide.region_0.1_spmd.clone.sunk | while | flops 65540 | bytes 262245 | solution.py:33
  142.2 0.9 fusion.81
  143.1 0.9 fusion.81
  144.0 0.9 fusion.81
  145.0 0.9 fusion.81
  145.9 0.9 fusion.81
  146.9 0.9 fusion.81
  147.8 0.9 fusion.81
  148.7 0.9 fusion.81
  149.7 0.9 fusion.81
  150.6 0.9 fusion.81
  151.5 0.9 fusion.81
  152.5 0.9 fusion.81
  153.4 0.9 fusion.81
  154.4 0.9 fusion.81
  155.3 0.9 fusion.81
  156.2 0.9 fusion.81
  157.2 0.9 fusion.81
  158.1 0.9 fusion.81
  159.0 0.9 fusion.81
  160.0 0.9 fusion.81
  160.9 0.9 fusion.81
  161.8 0.9 fusion.81
  162.8 0.9 fusion.81
  163.7 0.9 fusion.81
  164.7 0.9 fusion.81
  165.6 0.9 fusion.81
  166.5 0.9 fusion.81
  167.5 0.9 fusion.81
  168.4 0.9 fusion.81
  169.3 0.9 fusion.81
  170.3 0.9 fusion.81
  171.2 0.9 fusion.81
  172.2 2.1 collective-permute-start.2
  175.6 3.7 %collective-permute-start.3 = (f32[32,512]{1,0:T(8,128)S(1)}, f32[32,512]{1,0:T(8,128)S(1)}, u32[]{:S(2)}, u32[]{:S(2)}) collective-permute-start(f32[32,512]{1,0:T(8,128)S(1)} %slice_bitcast_fusion.1), channel_id=1, source_target_pairs={{0,1},{1,2},{2,3},{3,4},{4,5},{5,6},{6,7},{7,8},{8,9},{9,10},{10,1... | collective-permute-start | bytes 196616 | tf_op jit(solution)/shard_map/ppermute | solution.py:16
  180.6 4.7 %collective-permute-start.4 = (f32[32,512]{1,0:T(8,128)S(1)}, f32[32,512]{1,0:T(8,128)S(1)}, u32[]{:S(2)}, u32[]{:S(2)}) collective-permute-start(f32[32,512]{1,0:T(8,128)S(1)} %slice_bitcast_fusion), channel_id=1, source_target_pairs={{0,1},{1,2},{2,3},{3,4},{4,5},{5,6},{6,7},{7,8},{8,9},{9,10},{10,1... | collective-permute-start | bytes 196616 | tf_op jit(solution)/shard_map/ppermute | solution.py:16
  186.4 5.3 %fusion.5 = f32[8]{0:T(128)S(1)} fusion(f32[8,4,32,512]{3,2,1,0:T(8,128)S(1)} %copy-done, f32[4,32,512,1]{2,1,0,3:T(8,128)S(1)} %bitcast.54), kind=kOutput, calls=%fused_computation.7 | convolution fusion | flops 6291456 | bytes 2359328 | tf_op jit(solution)/shard_map/kabc,abc->k/dot_general | solution.py:99
  191.7 47.2 %psum.14 = f32[8]{0:T(128)S(1)} all-reduce(f32[8]{0:T(128)S(1)} %fusion.5), channel_id=1, replica_groups=mesh['tm'=32] {'tm'}, use_global_device_ids=true, to_apply=%region_2.3 | all-reduce | flops 8 | bytes 64 | tf_op jit(solution)/shard_map/psum | solution.py:100
  238.9 2.8 fusion.1
  242.4 39.6 %psum.15 = f32[]{:T(128)} all-reduce(f32[]{:T(128)} %multiply_reduce_fusion), channel_id=1, replica_groups=mesh['tm'=32] {'tm'}, use_global_device_ids=true, to_apply=%region_4.5 | all-reduce | flops 1 | bytes 8 | tf_op jit(solution)/shard_map/psum | solution.py:104
  (42 shorter events, 8.6 us)
Async XLA Ops:
  7.2 179.2 %copy-start = (f32[8,4,32,512]{3,2,1,0:T(8,128)S(1)}, f32[8,4,32,512]{3,2,1,0:T(8,128)}, u32[]{:S(2)}) copy-start(f32[8,4,32,512]{3,2,1,0:T(8,128)} %param.5) | copy-start | bytes 6291460
  7.2 6.5 %copy-start.2 = (f32[32,512]{1,0:T(8,128)S(1)}, f32[32,512]{1,0:T(8,128)}, u32[]{:S(2)}) copy-start(f32[32,512]{1,0:T(8,128)} %param.7) | copy-start | bytes 196612
  7.2 6.5 %copy-start.1 = (f32[4,32,512]{2,1,0:T(8,128)S(1)}, f32[4,32,512]{2,1,0:T(8,128)}, u32[]{:S(2)}) copy-start(f32[4,32,512]{2,1,0:T(8,128)} %param.6) | copy-start | bytes 786436
  7.2 76.5 %all-gather.5.cloned.1.call-start = ((), (), s32[]{:S(2)}) async-start(), calls=%async_computation | async-start | bytes 2162688 | tf_op jit(solution)/shard_map/all_gather | solution.py:21
  10.4 3.3 %collective-permute-start = (f32[32,512]{1,0:T(8,128)S(1)}, f32[32,512]{1,0:T(8,128)S(1)}, u32[]{:S(2)}, u32[]{:S(2)}) collective-permute-start(f32[32,512]{1,0:T(8,128)S(1)} %slice_bitcast_fusion.4), channel_id=1, source_target_pairs={{0,1},{1,2},{2,3},{3,4},{4,5},{5,6},{6,7},{7,8},{8,9},{9,10},{10,1... | collective-permute-start | bytes 196616 | tf_op jit(solution)/shard_map/ppermute | solution.py:16
  14.1 5.8 %collective-permute-start.1 = (f32[32,512]{1,0:T(8,128)S(1)}, f32[32,512]{1,0:T(8,128)S(1)}, u32[]{:S(2)}, u32[]{:S(2)}) collective-permute-start(f32[32,512]{1,0:T(8,128)S(1)} %get-tuple-element.168), channel_id=1, source_target_pairs={{0,1},{1,2},{2,3},{3,4},{4,5},{5,6},{6,7},{7,8},{8,9},{9,10},{10,1... | collective-permute-start | bytes 196616 | tf_op jit(solution)/shard_map/ppermute | solution.py:16
  20.8 121.4 %all-gather.7.cloned.1.call-start = ((), (), s32[]{:S(2)}) async-start(), calls=%async_computation.1 | async-start | bytes 2162688 | tf_op jit(solution)/shard_map/all_gather | solution.py:21
  172.2 3.0 %collective-permute-start.2 = (f32[32,512]{1,0:T(8,128)S(1)}, f32[32,512]{1,0:T(8,128)S(1)}, u32[]{:S(2)}, u32[]{:S(2)}) collective-permute-start(f32[32,512]{1,0:T(8,128)S(1)} %get-tuple-element.166), channel_id=1, source_target_pairs={{0,1},{1,2},{2,3},{3,4},{4,5},{5,6},{6,7},{7,8},{8,9},{9,10},{10,1... | collective-permute-start | bytes 196616 | tf_op jit(solution)/shard_map/ppermute | solution.py:16
  175.6 4.5 %collective-permute-start.3 = (f32[32,512]{1,0:T(8,128)S(1)}, f32[32,512]{1,0:T(8,128)S(1)}, u32[]{:S(2)}, u32[]{:S(2)}) collective-permute-start(f32[32,512]{1,0:T(8,128)S(1)} %slice_bitcast_fusion.1), channel_id=1, source_target_pairs={{0,1},{1,2},{2,3},{3,4},{4,5},{5,6},{6,7},{7,8},{8,9},{9,10},{10,1... | collective-permute-start | bytes 196616 | tf_op jit(solution)/shard_map/ppermute | solution.py:16
  180.6 61.2 %copy-start.3 = (f32[4,32,512]{2,1,0:T(8,128)}, f32[4,32,512]{2,1,0:T(8,128)S(1)}, u32[]{:S(2)}) copy-start(f32[4,32,512]{2,1,0:T(8,128)S(1)} %multiply_add_fusion) | copy-start | bytes 786436
  180.6 5.6 %collective-permute-start.4 = (f32[32,512]{1,0:T(8,128)S(1)}, f32[32,512]{1,0:T(8,128)S(1)}, u32[]{:S(2)}, u32[]{:S(2)}) collective-permute-start(f32[32,512]{1,0:T(8,128)S(1)} %slice_bitcast_fusion), channel_id=1, source_target_pairs={{0,1},{1,2},{2,3},{3,4},{4,5},{5,6},{6,7},{7,8},{8,9},{9,10},{10,1... | collective-permute-start | bytes 196616 | tf_op jit(solution)/shard_map/ppermute | solution.py:16
Sparse Core Ops, SparseCore 0:
  20.9 62.6 all-gather.4
  87.1 55.0 all-gather.6
where the time goes:
time: 293 us; the launch traced here: 291 us
  waiting for transfers between devices  126 us (43%)
  blocking collectives  86.8 us (30%)
  other arithmetic  36.6 us (12%)
  starting transfers between devices  17.9 us (6%)
  between operations  15 us (5%)
  matrix products  8.17 us (3%)
    all_gather x2, waiting for transfers between devices, entering(): everything = jax.tree.map(lambda part: lax.all_gather(part, axis), value)  121 us
    psum x1, blocking collectives, on_device(): weights = lax.psum(partial_dots, 'tm') / count_all  47.2 us
    psum x1, blocking collectives, on_device(): length = jnp.sqrt(lax.psum(jnp.sum(applied * applied), 'tm') / count_all)  39.6 us
    select_n x32, other arithmetic, lap(): return jax.tree.map(lambda a, b: jnp.where(reached, a, b), new, before)  29.3 us
    ppermute x5, starting transfers between devices, passed_along(): lax.ppermute(value, axis, [(source, source + steps) for source in range(i...  17.8 us
  transfers between devices with their start and end apart: 7, of which 7 were waited for; matrix products, arithmetic and copies ran while one was open for 0% of the time, Pallas kernels for 0%

commit v1 on v0

v1 whole, which is shorter than its diff:
```python
import functools

import jax
import jax.numpy as jnp
from jax import lax
from jax.experimental import pallas as pl
from jax.experimental.pallas import tpu as pltpu
from jax.sharding import PartitionSpec as P

OMEGA = 0.7
FLOOR = 0.25
LANES = 128
MESH = pl.DeviceIdType.MESH


def to_rows(slab):
    return jnp.concatenate(
        [slab[:, at : at + LANES] for at in range(0, slab.shape[1], LANES)], axis=0
    )


def from_rows(rows, sx):
    return jnp.concatenate(
        [rows[at : at + sx] for at in range(0, rows.shape[0], sx)], axis=1
    )


def folded(x):
    parts = [
        x[a : a + 8, b : b + LANES]
        for a in range(0, x.shape[0], 8)
        for b in range(0, x.shape[1], LANES)
    ]
    while len(parts) > 1:
        parts = [parts[i] + parts[i + 1] for i in range(0, len(parts) - 1, 2)] + (
            [parts[-1]] if len(parts) % 2 else []
        )
    return parts[0]


def total(x):
    return jnp.sum(jnp.sum(folded(x), axis=0, keepdims=True), axis=1, keepdims=True)


def kernel(
    n,
    count_all,
    basis_hbm,
    vec_hbm,
    cond_hbm,
    pre_hbm,
    nxt_hbm,
    coef_ref,
    basis,
    vec,
    cond,
    pre,
    nxt,
    zout,
    zin,
    sout,
    sin,
    dchunk,
    halo_out,
    halo_in,
    late_out,
    late_in,
    part_out,
    part_in,
    load_sem,
    store_sem,
    z_sem,
    s_sem,
    h_sem,
    l_sem,
    p_sem,
):
    me = lax.axis_index("tm")
    members, m, sx, sy = basis.shape

    load_c = pltpu.make_async_copy(cond_hbm, cond, load_sem.at[0])
    load_v = pltpu.make_async_copy(vec_hbm, vec, load_sem.at[1])
    load_b = pltpu.make_async_copy(basis_hbm, basis, load_sem.at[2])
    load_c.start()
    load_v.start()
    load_b.start()

    barrier = pltpu.get_barrier_semaphore()

    def peer_of(step):
        return lax.rem(me + step, n)

    def greet(step, _):
        pl.semaphore_signal(barrier, inc=1, device_id=(peer_of(step),), device_id_type=MESH)
        return 0

    lax.fori_loop(1, n, greet, 0, unroll=n <= 32)

    def to_all(pick, into, sems):
        def send(step, _):
            peer = peer_of(step)
            pltpu.make_async_remote_copy(
                src_ref=pick(peer),
                dst_ref=into.at[me],
                send_sem=sems.at[0],
                recv_sem=sems.at[1],
                device_id=(peer,),
                device_id_type=MESH,
            ).start()
            return 0

        lax.fori_loop(1, n, send, 0, unroll=n <= 32)

    def all_of(buffer, sems):
        some = buffer.at[pl.ds(0, n - 1)]
        return pltpu.make_async_remote_copy(
            src_ref=some,
            dst_ref=some,
            send_sem=sems.at[0],
            recv_sem=sems.at[1],
            device_id=(peer_of(1),),
            device_id_type=MESH,
        )

    def to_next(src, dst, sems):
        return pltpu.make_async_remote_copy(
            src_ref=src,
            dst_ref=dst,
            send_sem=sems.at[0],
            recv_sem=sems.at[1],
            device_id=(peer_of(1),),
            device_id_type=MESH,
        )

    load_c.wait()
    c0 = cond[...]
    diag = [1.0 + 4.0 * c0, 1.0 + 8.0 * c0, 1.0 + 16.0 * c0]
    inv = [1.0 / d for d in diag]
    con = [c0, 2.0 * c0]
    row = lax.broadcasted_iota(jnp.int32, (sx, sy), 0)
    col = lax.broadcasted_iota(jnp.int32, (sx, sy), 1)

    def beside(v):
        up = jnp.where(row == 0, 0.0, pltpu.roll(v, 1, 0))
        down = jnp.where(row == sx - 1, 0.0, pltpu.roll(v, sx - 1, 0))
        left = jnp.where(col == 0, 0.0, pltpu.roll(v, 1, 1))
        right = jnp.where(col == sy - 1, 0.0, pltpu.roll(v, sy - 1, 1))
        return (up + down) + (left + right)

    def K(v, level):
        return diag[level] * v - con[level] * beside(v)

    def B(r, level):
        return (r + con[level] * beside(r * inv[level])) * (OMEGA * inv[level])

    @pl.when(me == 0)
    def _():
        halo_in[...] = jnp.zeros_like(halo_in)
        late_in[...] = jnp.zeros_like(late_in)

    load_v.wait()
    r = [vec[i] for i in range(m)]
    u = [B(r[i], 0) for i in range(m)]
    s = [r[0] - K(u[0], 0)] + [r[i] - K(u[i], 0) + u[i - 1] for i in range(1, m)]
    cl = [s[0] + s[1], s[2] + s[3]]
    v0 = B(cl[0], 1)
    v1 = B(cl[1], 1)
    t0 = cl[0] - K(v0, 1)
    t1 = cl[1] - K(v1, 1) + v0
    q_next = B(u[3], 1)
    x_next = u[3] - K(q_next, 1) + q_next + v1
    dl = (t0 + t1) * inv[2]
    zout[...] = to_rows(dl + x_next).reshape(zout.shape)
    dchunk[...] = to_rows(inv[2]).reshape(dchunk.shape)
    halo_out[0] = u[3]
    halo_out[1] = v1

    pl.semaphore_wait(barrier, n - 1)
    to_all(lambda peer: zout.at[peer], zin, z_sem)

    halo = to_next(halo_out, halo_in, h_sem)

    @pl.when(me < n - 1)
    def _():
        halo.start()

    zin[me] = zout[me]
    dmine = dchunk[me]
    all_of(zin, z_sem).wait_recv()

    def advance(k, state):
        sout[k] = state
        return (zin[k] + state) * dmine

    lax.fori_loop(0, n, advance, jnp.zeros_like(dmine), unroll=n <= 32)
    to_all(lambda peer: sout.at[peer], sin, s_sem)
    sin[me] = sout[me]

    @pl.when(me > 0)
    def _():
        halo.wait_recv()

    p = halo_in[0]
    q = B(p, 1)
    a = p - K(q, 1) + halo_in[1]
    x_mine = a + q
    e1 = v1 + B(t1 + q, 1)
    n2 = u[2] + e1
    n3 = u[3] + e1
    res3 = n3 + B(r[3] - K(n3, 0) + n2, 0)
    late_out[0] = n3
    late_out[1] = res3
    late = to_next(late_out, late_in, l_sem)

    @pl.when(me < n - 1)
    def _():
        late.start()

    e0 = v0 + q + B(t0 + a, 1)
    n0 = u[0] + e0
    n1 = u[1] + e0
    res1 = n1 + B(r[1] - K(n1, 0) + n0, 0)
    res2 = n2 + B(r[2] - K(n2, 0) + n1, 0)
    m0 = r[0] - K(n0, 0)

    load_b.wait()
    lane = lax.broadcasted_iota(jnp.int32, (1, LANES), 1)
    part = jnp.zeros((1, LANES), jnp.float32)
    for j in range(members):
        square = basis[j, 0] * basis[j, 0]
        for i in range(1, m):
            square += basis[j, i] * basis[j, i]
        part = jnp.where(lane == members + 1 + j, total(square), part)

    @pl.when(me > 0)
    def _():
        late.wait_recv()

    res0 = n0 + B(m0 + late_in[0], 0)
    resp = late_in[1]

    all_of(sin, s_sem).wait_recv()
    entering = from_rows(sin[...].reshape(sx * sy // LANES, LANES), sx)
    e = dl + entering
    ep = diag[2] * entering - x_mine
    ke = K(e, 1)
    f0 = e - B(ke - ep, 1)
    f1 = e - B(ke - e, 1)
    fp = ep - B(K(ep, 1) - ep, 1)
    k0 = K(f0, 0)
    k1 = K(f1, 0)
    res0 += f0 - B(k0 - fp, 0)
    res1 += f0 - B(k0 - f0, 0)
    res2 += f1 - B(k1 - f0, 0)
    res3 += f1 - B(k1 - f1, 0)
    resp += fp - B(K(fp, 0) - fp, 0)
    res = [res0, res1, res2, res3]
    for i in range(m):
        pre[i] = res[i]
    store_p = pltpu.make_async_copy(pre, pre_hbm, store_sem.at[0])
    store_p.start()

    w = [K(res[i], 0) - (res[i - 1] if i else resp) for i in range(m)]
    for j in range(members):
        dot = w[0] * basis[j, 0]
        for i in range(1, m):
            dot += w[i] * basis[j, i]
        part = jnp.where(lane == j, total(dot), part)
    square = w[0] * w[0]
    for i in range(1, m):
        square += w[i] * w[i]
    part = jnp.where(lane == members, total(square), part)
    part_out[...] = part
    to_all(lambda peer: part_out, part_in, p_sem)
    part_in[me] = part
    all_of(part_in, p_sem).wait_recv()
    sums = jnp.sum(part_in[...], axis=0) * (1.0 / count_all)

    weights = [sums[:, j : j + 1] for j in range(members)]
    left = sums[:, members : members + 1]
    for j in range(members):
        gram = sums[:, members + 1 + j : members + 2 + j]
        left -= weights[j] * weights[j] * (2.0 - gram)
    length = jnp.sqrt(jnp.maximum(left, 0.0))
    scale = 1.0 / jnp.maximum(length, FLOOR)
    for i in range(m):
        out = w[i]
        for j in range(members):
            out -= weights[j] * basis[j, i]
        nxt[i] = out * scale
    store_n = pltpu.make_async_copy(nxt, nxt_hbm, store_sem.at[1])
    store_n.start()
    for j in range(members):
        coef_ref[j] = weights[j][0, 0]
    coef_ref[members] = length[0, 0]

    all_of(zin, z_sem).wait_send()
    all_of(sin, s_sem).wait_send()
    all_of(part_in, p_sem).wait_send()

    @pl.when(me < n - 1)
    def _():
        halo.wait_send()
        late.wait_send()

    store_p.wait()
    store_n.wait()


def solution(mesh):
    n = mesh.shape["tm"]

    def on_device(krylov_basis, vector, conductance):
        members, m, sx, sy = krylov_basis.shape
        assert m == 4
        rows = sx * sy // LANES // n
        chunk = pltpu.VMEM((n, rows, LANES), jnp.float32)
        slabs = lambda k: pltpu.VMEM((k, sx, sy), jnp.float32)
        pair = pltpu.SemaphoreType.DMA((2,))
        anywhere = pl.BlockSpec(memory_space=pl.ANY)
        return pl.pallas_call(
            functools.partial(kernel, n, m * n * sx * sy),
            out_shape=(
                jax.ShapeDtypeStruct(vector.shape, jnp.float32),
                jax.ShapeDtypeStruct(vector.shape, jnp.float32),
                jax.ShapeDtypeStruct((members + 1,), jnp.float32),
            ),
            in_specs=[anywhere] * 3,
            out_specs=(anywhere, anywhere, pl.BlockSpec(memory_space=pltpu.SMEM)),
            scratch_shapes=[
                pltpu.VMEM(krylov_basis.shape, jnp.float32),
                slabs(m),
                pltpu.VMEM((sx, sy), jnp.float32),
                slabs(m),
                slabs(m),
                chunk,
                chunk,
                chunk,
                chunk,
                chunk,
                slabs(2),
                slabs(2),
                slabs(2),
                slabs(2),
                pltpu.VMEM((1, LANES), jnp.float32),
                pltpu.VMEM((n, 1, LANES), jnp.float32),
                pltpu.SemaphoreType.DMA((3,)),
                pair,
                pair,
                pair,
                pair,
                pair,
                pair,
            ],
            compiler_params=pltpu.CompilerParams(collective_id=0, has_side_effects=True),
            name="arnoldi_step",
        )(krylov_basis, vector, conductance)

    return jax.shard_map(
        on_device,
        mesh=mesh,
        in_specs=(P(None, "tm", None, None), P("tm", None, None), P()),
        out_specs=(P("tm", None, None), P("tm", None, None), P()),
        check_vma=False,
    )
```

time: 293 us -> 28.6 us (0.10)
  waiting for transfers between devices: 126 us -> 0 us
  blocking collectives: 86.8 us -> 0 us
  other arithmetic: 36.6 us -> 0 us
  Pallas kernels: 0 us -> 23.3 us
  starting transfers between devices: 17.9 us -> 0 us
  between operations: 15 us -> 0.64 us
  matrix products: 8.17 us -> 0 us
  local copies, waits for them, and re-layouts: 0.11 us -> 4.45 us
    all_gather x2 -> x0, waiting for transfers between devices: 121 us -> none  [entering(): everything = jax.tree.map(lambda part: lax.all_gather(part, axis), value)]
    psum x2 -> x0, blocking collectives: 86.8 us -> none  [the longest x1 47.2 us: on_device(): weights = lax.psum(partial_dots, 'tm') / count_all]
    select_n x32 -> x0, other arithmetic: 29.3 us -> none  [lap(): return jax.tree.map(lambda a, b: jnp.where(reached, a, b), new, before)]
    pallas_call x0 -> x1, Pallas kernels: none -> 23.3 us  [on_device(): pl.pallas_call(functools.partial(kernel, n, m * n * sx * sy), out_shape=(...]
    ppermute x5 -> x0, starting transfers between devices: 17.8 us -> none  [passed_along(): lax.ppermute(value, axis, [(source, source + steps) for source in range(i...]
    dot_general x2 -> x0, matrix products: 8.17 us -> none  [the longest x1 5.33 us: on_device(): jnp.einsum('kabc,abc->k', krylov_basis, applied, precision=lax.Precision....]
    unnamed x8 -> x3, local copies, waits for them, and re-layouts: 0.03 us -> 4.45 us
    ppermute x5 -> x0, waiting for transfers between devices: 4.34 us -> none  [passed_along(): lax.ppermute(value, axis, [(source, source + steps) for source in range(i...]
  transfers between devices with their start and end apart: 7 -> 0, of which waited for: 7 -> 0; matrix products, arithmetic and copies ran while one was open for 0% -> 0% of each run, Pallas kernels for 0% -> 0%
where the time goes in v1:
time: 28.6 us; the launch traced here: 28.4 us
  Pallas kernels  23.3 us (81%)
  local copies, waits for them, and re-layouts  4.45 us (16%)
  between operations  0.64 us (2%)
    pallas_call x1, Pallas kernels, on_device(): pl.pallas_call(functools.partial(kernel, n, m * n * sx * sy), out_shape=(...  23.3 us
    unnamed x3, local copies, waits for them, and re-layouts  4.45 us

profile of v1, /device:TPU:0, one launch (start us, length us, event | category | flops | bytes accessed | tf_op | source)
XLA Modules:
  0.0 28.4 jit_solution(8066951724729587444)
XLA Ops:
  0.6 23.3 %arnoldi_step.1 = (f32[4,32,512]{2,1,0:T(8,128)}, f32[4,32,512]{2,1,0:T(8,128)}, f32[9]{0:T(128)}) custom-call(f32[8,4,32,512]{3,2,1,0:T(8,128)} %basis_hbm.1, f32[4,32,512]{2,1,0:T(8,128)} %vec_hbm.1, f32[32,512]{1,0:T(8,128)} %cond_hbm.1), custom_call_target="tpu_custom_call" | custom-call | tf_op jit(solution)/shard_map/arnoldi_step/pallas_call | solution.py:321
  23.9 1.7 %copy.9 = f32[4,32,512]{2,1,0:T(8,128)} copy(f32[4,32,512]{2,1,0:T(8,128)} %get-tuple-element.6) | data formatting | bytes 524288
  25.6 1.7 %copy.10 = f32[4,32,512]{2,1,0:T(8,128)} copy(f32[4,32,512]{2,1,0:T(8,128)} %get-tuple-element.7) | data formatting | bytes 524288
  27.3 1.1 %copy.11 = f32[9]{0:T(128)} copy(f32[9]{0:T(128)} %get-tuple-element.8) | data formatting | bytes 72

commit v2 on v1

--- a/solution.py
+++ b/solution.py
@@ -48,14 +48,12 @@
     basis_hbm,
     vec_hbm,
     cond_hbm,
-    pre_hbm,
-    nxt_hbm,
-    coef_ref,
+    pre,
+    w_ref,
+    sums_ref,
     basis,
     vec,
     cond,
-    pre,
-    nxt,
     zout,
     zin,
     sout,
@@ -68,7 +66,6 @@
     part_out,
     part_in,
     load_sem,
-    store_sem,
     z_sem,
     s_sem,
     h_sem,
@@ -257,10 +254,10 @@
     res = [res0, res1, res2, res3]
     for i in range(m):
         pre[i] = res[i]
-    store_p = pltpu.make_async_copy(pre, pre_hbm, store_sem.at[0])
-    store_p.start()
 
     w = [K(res[i], 0) - (res[i - 1] if i else resp) for i in range(m)]
+    for i in range(m):
+        w_ref[i] = w[i]
     for j in range(members):
         dot = w[0] * basis[j, 0]
         for i in range(1, m):
@@ -274,8 +271,23 @@
     to_all(lambda peer: part_out, part_in, p_sem)
     part_in[me] = part
     all_of(part_in, p_sem).wait_recv()
-    sums = jnp.sum(part_in[...], axis=0) * (1.0 / count_all)
-
+    sums_ref[...] = jnp.sum(part_in[...], axis=0) * (1.0 / count_all)
+
+    all_of(zin, z_sem).wait_send()
+    all_of(sin, s_sem).wait_send()
+    all_of(part_in, p_sem).wait_send()
+
+    @pl.when(me < n - 1)
+    def _():
+        halo.wait_send()
+        late.wait_send()
+
+
+def finish(pre, w, sums_ref, basis, pre_hbm, nxt_hbm, coef_ref, nxt, store_sem):
+    members, m = basis.shape[:2]
+    store_p = pltpu.make_async_copy(pre, pre_hbm, store_sem.at[0])
+    store_p.start()
+    sums = sums_ref[...]
     weights = [sums[:, j : j + 1] for j in range(members)]
     left = sums[:, members : members + 1]
     for j in range(members):
@@ -283,28 +295,20 @@
         left -= weights[j] * weights[j] * (2.0 - gram)
     length = jnp.sqrt(jnp.maximum(left, 0.0))
     scale = 1.0 / jnp.maximum(length, FLOOR)
+    stores = []
     for i in range(m):
         out = w[i]
         for j in range(members):
             out -= weights[j] * basis[j, i]
         nxt[i] = out * scale
-    store_n = pltpu.make_async_copy(nxt, nxt_hbm, store_sem.at[1])
-    store_n.start()
+        stores.append(pltpu.make_async_copy(nxt.at[i], nxt_hbm.at[i], store_sem.at[i + 1]))
+        stores[-1].start()
     for j in range(members):
         coef_ref[j] = weights[j][0, 0]
     coef_ref[members] = length[0, 0]
-
-    all_of(zin, z_sem).wait_send()
-    all_of(sin, s_sem).wait_send()
-    all_of(part_in, p_sem).wait_send()
-
-    @pl.when(me < n - 1)
-    def _():
-        halo.wait_send()
-        late.wait_send()
-
     store_p.wait()
-    store_n.wait()
+    for store in stores:
+        store.wait()
 
 
 def solution(mesh):
@@ -318,21 +322,20 @@
         slabs = lambda k: pltpu.VMEM((k, sx, sy), jnp.float32)
         pair = pltpu.SemaphoreType.DMA((2,))
         anywhere = pl.BlockSpec(memory_space=pl.ANY)
-        return pl.pallas_call(
+        inside = pl.BlockSpec(memory_space=pltpu.VMEM)
+        pre, w, sums, basis = pl.pallas_call(
             functools.partial(kernel, n, m * n * sx * sy),
             out_shape=(
-                jax.ShapeDtypeStruct(vector.shape, jnp.float32),
-                jax.ShapeDtypeStruct(vector.shape, jnp.float32),
-                jax.ShapeDtypeStruct((members + 1,), jnp.float32),
+                pltpu.VMEM(vector.shape, jnp.float32),
+                pltpu.VMEM(vector.shape, jnp.float32),
+                pltpu.VMEM((1, LANES), jnp.float32),
+                pltpu.VMEM(krylov_basis.shape, jnp.float32),
             ),
             in_specs=[anywhere] * 3,
-            out_specs=(anywhere, anywhere, pl.BlockSpec(memory_space=pltpu.SMEM)),
+            out_specs=(inside,) * 4,
             scratch_shapes=[
-                pltpu.VMEM(krylov_basis.shape, jnp.float32),
                 slabs(m),
                 pltpu.VMEM((sx, sy), jnp.float32),
-                slabs(m),
-                slabs(m),
                 chunk,
                 chunk,
                 chunk,
@@ -350,11 +353,23 @@
                 pair,
                 pair,
                 pair,
-                pair,
             ],
             compiler_params=pltpu.CompilerParams(collective_id=0, has_side_effects=True),
             name="arnoldi_step",
         )(krylov_basis, vector, conductance)
+        held = [pltpu.with_memory_space_constraint(x, pltpu.VMEM) for x in (pre, w, sums, basis)]
+        return pl.pallas_call(
+            finish,
+            out_shape=(
+                jax.ShapeDtypeStruct(vector.shape, jnp.float32),
+                jax.ShapeDtypeStruct(vector.shape, jnp.float32),
+                jax.ShapeDtypeStruct((members + 1,), jnp.float32),
+            ),
+            in_specs=[inside] * 4,
+            out_specs=(anywhere, anywhere, pl.BlockSpec(memory_space=pltpu.SMEM)),
+            scratch_shapes=[slabs(m), pltpu.SemaphoreType.DMA((m + 1,))],
+            name="next_vector",
+        )(*held)
 
     return jax.shard_map(
         on_device,

time: 28.6 us -> 24.1 us (0.84)
  local copies, waits for them, and re-layouts: 4.45 us -> 0 us
    unnamed x3 -> x0, local copies, waits for them, and re-layouts: 4.45 us -> none
    pallas_call x0 -> x1, Pallas kernels: none -> 1.56 us  [on_device(): pl.pallas_call(finish, out_shape=(jax.ShapeDtypeStruct(vector.shape, jnp....]
    pallas_call x1, Pallas kernels: 23.3 us -> 21.8 us  [on_device(): pl.pallas_call(functools.partial(kernel, n, m * n * sx * sy), out_shape=(...]
where the time goes in v2:
time: 24.1 us; the launch traced here: 24 us
  Pallas kernels  23.3 us (97%)
  between operations  0.64 us (3%)
    pallas_call x1, Pallas kernels, on_device(): pl.pallas_call(functools.partial(kernel, n, m * n * sx * sy), out_shape=(...  21.8 us
    pallas_call x1, Pallas kernels, on_device(): pl.pallas_call(finish, out_shape=(jax.ShapeDtypeStruct(vector.shape, jnp....  1.56 us

profile of v2, /device:TPU:0, one launch (start us, length us, event | category | flops | bytes accessed | tf_op | source)
XLA Modules:
  0.0 24.0 jit_solution(10017263929490729786)
XLA Ops:
  0.6 21.8 %arnoldi_step.1 = (f32[4,32,512]{2,1,0:T(8,128)S(1)}, f32[4,32,512]{2,1,0:T(8,128)S(1)}, f32[1,128]{1,0:T(1,128)S(1)}, f32[8,4,32,512]{3,2,1,0:T(8,128)S(1)}) custom-call(f32[8,4,32,512]{3,2,1,0:T(8,128)} %basis_hbm.1, f32[4,32,512]{2,1,0:T(8,128)} %vec_hbm.1, f32[32,512]{1,0:T(8,128)} %cond_hbm.1), custom_call_target="tpu_custom_call" | custom-call | tf_op jit(solution)/shard_map/arnoldi_step/pallas_call | solution.py:326
  22.4 1.6 %next_vector.1 = (f32[4,32,512]{2,1,0:T(8,128)}, f32[4,32,512]{2,1,0:T(8,128)}, f32[9]{0:T(128)}) custom-call(f32[4,32,512]{2,1,0:T(8,128)S(1)} %get-tuple-element.7.pre, f32[4,32,512]{2,1,0:T(8,128)S(1)} %get-tuple-element.8.w, f32[1,128]{1,0:T(1,128)S(1)} %get-tuple-element.9.sums_ref, f32[8,4,32,512]{3,2,1,0:T(8,128)S(1)} %get-tuple-element.10.basis), custom_call_target="tpu_custom_call" | custom-call | tf_op jit(solution)/shard_map/next_vector/pallas_call | solution.py:361

commit v3 on v2

--- a/solution.py
+++ b/solution.py
@@ -98,7 +98,7 @@
             peer = peer_of(step)
             pltpu.make_async_remote_copy(
                 src_ref=pick(peer),
-                dst_ref=into.at[me],
+                dst_ref=into,
                 send_sem=sems.at[0],
                 recv_sem=sems.at[1],
                 device_id=(peer,),
@@ -108,8 +108,8 @@
 
         lax.fori_loop(1, n, send, 0, unroll=n <= 32)
 
-    def all_of(buffer, sems):
-        some = buffer.at[pl.ds(0, n - 1)]
+    def all_of(buffer, count, sems):
+        some = buffer.at[pl.ds(0, count)]
         return pltpu.make_async_remote_copy(
             src_ref=some,
             dst_ref=some,
@@ -172,8 +172,30 @@
     halo_out[0] = u[3]
     halo_out[1] = v1
 
+    owners = n // 2
+    first = n // 4
+    mine = lax.rem(me - first + n, owners)
+    owner = jnp.logical_and(me >= first, me < first + owners)
+
     pl.semaphore_wait(barrier, n - 1)
-    to_all(lambda peer: zout.at[peer], zin, z_sem)
+
+    def to_owner(step, _):
+        chunk = lax.rem(mine + step, owners)
+        pltpu.make_async_remote_copy(
+            src_ref=zout.at[chunk],
+            dst_ref=zin.at[me],
+            send_sem=z_sem.at[0],
+            recv_sem=z_sem.at[1],
+            device_id=(first + chunk,),
+            device_id_type=MESH,
+        ).start()
+        return 0
+
+    @pl.when(jnp.logical_not(owner))
+    def _():
+        to_owner(0, 0)
+
+    lax.fori_loop(1, owners, to_owner, 0, unroll=n <= 32)
 
     halo = to_next(halo_out, halo_in, h_sem)
 
@@ -181,17 +203,19 @@
     def _():
         halo.start()
 
-    zin[me] = zout[me]
-    dmine = dchunk[me]
-    all_of(zin, z_sem).wait_recv()
-
-    def advance(k, state):
-        sout[k] = state
-        return (zin[k] + state) * dmine
-
-    lax.fori_loop(0, n, advance, jnp.zeros_like(dmine), unroll=n <= 32)
-    to_all(lambda peer: sout.at[peer], sin, s_sem)
-    sin[me] = sout[me]
+    @pl.when(owner)
+    def _():
+        zin[me] = zout[mine]
+        dmine = dchunk[mine]
+        all_of(zin, n - 1, z_sem).wait_recv()
+
+        def advance(k, state):
+            sout[k] = state
+            return (zin[k] + state) * dmine
+
+        lax.fori_loop(0, n, advance, jnp.zeros_like(dmine), unroll=n <= 32)
+        to_all(lambda peer: sout.at[peer], sin.at[mine], s_sem)
+        sin[mine] = sout[me]
 
     @pl.when(me > 0)
     def _():
@@ -236,7 +260,14 @@
     res0 = n0 + B(m0 + late_in[0], 0)
     resp = late_in[1]
 
-    all_of(sin, s_sem).wait_recv()
+    @pl.when(owner)
+    def _():
+        all_of(sin, owners - 1, s_sem).wait_recv()
+
+    @pl.when(jnp.logical_not(owner))
+    def _():
+        all_of(sin, owners, s_sem).wait_recv()
+
     entering = from_rows(sin[...].reshape(sx * sy // LANES, LANES), sx)
     e = dl + entering
     ep = diag[2] * entering - x_mine
@@ -268,14 +299,21 @@
         square += w[i] * w[i]
     part = jnp.where(lane == members, total(square), part)
     part_out[...] = part
-    to_all(lambda peer: part_out, part_in, p_sem)
+    to_all(lambda peer: part_out, part_in.at[me], p_sem)
     part_in[me] = part
-    all_of(part_in, p_sem).wait_recv()
+    all_of(part_in, n - 1, p_sem).wait_recv()
     sums_ref[...] = jnp.sum(part_in[...], axis=0) * (1.0 / count_all)
 
-    all_of(zin, z_sem).wait_send()
-    all_of(sin, s_sem).wait_send()
-    all_of(part_in, p_sem).wait_send()
+    @pl.when(owner)
+    def _():
+        all_of(zout, owners - 1, z_sem).wait_send()
+        all_of(sout, n - 1, s_sem).wait_send()
+
+    @pl.when(jnp.logical_not(owner))
+    def _():
+        all_of(zout, owners, z_sem).wait_send()
+
+    all_of(part_in, n - 1, p_sem).wait_send()
 
     @pl.when(me < n - 1)
     def _():
@@ -317,8 +355,10 @@
     def on_device(krylov_basis, vector, conductance):
         members, m, sx, sy = krylov_basis.shape
         assert m == 4
-        rows = sx * sy // LANES // n
-        chunk = pltpu.VMEM((n, rows, LANES), jnp.float32)
+        owners = n // 2
+        rows = sx * sy // LANES // owners
+        chunk = pltpu.VMEM((owners, rows, LANES), jnp.float32)
+        steps = pltpu.VMEM((n, rows, LANES), jnp.float32)
         slabs = lambda k: pltpu.VMEM((k, sx, sy), jnp.float32)
         pair = pltpu.SemaphoreType.DMA((2,))
         anywhere = pl.BlockSpec(memory_space=pl.ANY)
@@ -337,8 +377,8 @@
                 slabs(m),
                 pltpu.VMEM((sx, sy), jnp.float32),
                 chunk,
-                chunk,
-                chunk,
+                steps,
+                steps,
                 chunk,
                 chunk,
                 slabs(2),

time: 24.1 us -> 24.6 us (1.021)
  Pallas kernels: 23.3 us -> 23.8 us
    pallas_call x1, Pallas kernels: 21.8 us -> 22.3 us  [on_device(): pl.pallas_call(functools.partial(kernel, n, m * n * sx * sy), out_shape=(...]
where the time goes in v3:
time: 24.6 us; the launch traced here: 24.4 us
  Pallas kernels  23.8 us (97%)
  between operations  0.64 us (3%)
    pallas_call x1, Pallas kernels, on_device(): pl.pallas_call(functools.partial(kernel, n, m * n * sx * sy), out_shape=(...  22.3 us
    pallas_call x1, Pallas kernels, on_device(): pl.pallas_call(finish, out_shape=(jax.ShapeDtypeStruct(vector.shape, jnp....  1.56 us

profile of v3, /device:TPU:0, one launch (start us, length us, event | category | flops | bytes accessed | tf_op | source)
XLA Modules:
  0.0 24.4 jit_solution(3431413112341053000)
XLA Ops:
  0.6 22.3 %arnoldi_step.1 = (f32[4,32,512]{2,1,0:T(8,128)S(1)}, f32[4,32,512]{2,1,0:T(8,128)S(1)}, f32[1,128]{1,0:T(1,128)S(1)}, f32[8,4,32,512]{3,2,1,0:T(8,128)S(1)}) custom-call(f32[8,4,32,512]{3,2,1,0:T(8,128)} %basis_hbm.1, f32[4,32,512]{2,1,0:T(8,128)} %vec_hbm.1, f32[32,512]{1,0:T(8,128)} %cond_hbm.1), custom_call_target="tpu_custom_call" | custom-call | tf_op jit(solution)/shard_map/arnoldi_step/pallas_call | solution.py:366
  22.9 1.6 %next_vector.1 = (f32[4,32,512]{2,1,0:T(8,128)}, f32[4,32,512]{2,1,0:T(8,128)}, f32[9]{0:T(128)}) custom-call(f32[4,32,512]{2,1,0:T(8,128)S(1)} %get-tuple-element.7.pre, f32[4,32,512]{2,1,0:T(8,128)S(1)} %get-tuple-element.8.w, f32[1,128]{1,0:T(1,128)S(1)} %get-tuple-element.9.sums_ref, f32[8,4,32,512]{3,2,1,0:T(8,128)S(1)} %get-tuple-element.10.basis), custom_call_target="tpu_custom_call" | custom-call | tf_op jit(solution)/shard_map/next_vector/pallas_call | solution.py:401
